TPU v7x, 32 devices: a whole 2x2x4 slice. The times are simulated.
32 devices in a mesh: dp: 4 (over z), tensor: 8 (over y, x, core).
Axes of the slice: x: 2, y: 2, z: 4, core: 2. Of those that a mesh axis runs over, the one named last changes fastest.
Arguments:
- inputs: bfloat16 [8192, 2048], P(('dp', 'tensor')), may hold values from -6 to 6
- doc_lengths: int32 [8, 8], P('dp'), may hold values from 1 to 512, 1024 in all within a row
- attn_gain: bfloat16 [2048], replicated, may hold values from 0.099609375 to 1.8984375
- attn_shift: bfloat16 [2048], replicated, may hold values from -1.5 to 1.5
- qkv_weight: bfloat16 [2048, 3, 2048], P(None, None, 'tensor'), may hold values from -0.1875 to 0.1875
- qv_bias: bfloat16 [2, 2048], P(None, 'tensor'), may hold values from -2.5 to 2.5
- out_weight: bfloat16 [2048, 2048], P('tensor'), may hold values from -0.5 to 0.5
- out_bias: bfloat16 [2048], replicated, may hold values from -1.5 to 1.5
- mlp_gain: bfloat16 [2048], replicated, may hold values from 0.099609375 to 1.8984375
- mlp_shift: bfloat16 [2048], replicated, may hold values from -1.5 to 1.5
- up_weight: bfloat16 [2048, 8192], P(None, 'tensor'), may hold values from -0.125 to 0.125
- up_bias: bfloat16 [8192], P('tensor'), may hold values from -2.5 to 2.5
- down_weight: bfloat16 [8192, 2048], P('tensor'), may hold values from -0.09375 to 0.09375
- down_bias: bfloat16 [2048], replicated, may hold values from -1.5 to 1.5
- out_grad: bfloat16 [8192, 2048], P(('dp', 'tensor')), may hold values from -6 to 6
Outputs:
- outputs: bfloat16 [8192, 2048], P(('dp', 'tensor'))
- input_grad: float32 [8192, 2048], P(('dp', 'tensor'))
- attn_gain_grad: float32 [2048], replicated
- attn_shift_grad: float32 [2048], replicated
- qkv_weight_grad: float32 [2048, 3, 2048], P(None, None, 'tensor')
- qv_bias_grad: float32 [2, 2048], P(None, 'tensor')
- out_weight_grad: float32 [2048, 2048], P('tensor')
- out_bias_grad: float32 [2048], replicated
- mlp_gain_grad: float32 [2048], replicated
- mlp_shift_grad: float32 [2048], replicated
- up_weight_grad: float32 [2048, 8192], P(None, 'tensor')
- up_bias_grad: float32 [8192], P('tensor')
- down_weight_grad: float32 [8192, 2048], P('tensor')
- down_bias_grad: float32 [2048], replicated
Inputs may be any that keep to these rules, and one draw needn't show every extreme that they name: `doc_lengths`: each row's 8 lengths sum to 1024, and the longest document of every row has exactly 512 tokens.
All inputs are finite; a program needn't handle non-finite values.
Results may differ from a plain program's by a relative error of at most 0.012.
The roundings to bfloat16 on the way count: a program that leaves them out, or rounds other values in their place, can miss the bound.
Values may be sent and summed in bfloat16 or wider, within the bound.
A program may use at most 192 MiB of HBM per device.

v0:
```python
import jax
import jax.numpy as jnp
from jax import lax
from jax.sharding import PartitionSpec as P

HD = 128
NORM_EPS = 1e-05


def layer_norm(values, gain_vec, shift_vec):
    row_mean = jnp.mean(values, axis=-1, keepdims=True)
    centred = values - row_mean
    variance = jnp.mean(centred * centred, axis=-1, keepdims=True)
    return centred * lax.rsqrt(variance + NORM_EPS) * gain_vec + shift_vec


def allowed_pairs(lengths, length):
    doc_ends = jnp.cumsum(lengths, dtype=jnp.int32)
    positions = jnp.arange(length, dtype=jnp.int32)
    doc_ids = jnp.sum((positions[:, None] >= doc_ends[None, :]).astype(jnp.int32), axis=1)
    return (doc_ids[:, None] == doc_ids[None, :]) & (positions[None, :] <= positions[:, None])


def row_scores(query_rows, key_rows, lengths):
    raw_scores = jnp.einsum(
        "qhd,khd->hqk", query_rows, key_rows, preferred_element_type=jnp.float32
    )
    raw_scores = raw_scores * query_rows.shape[2] ** (-0.5)
    return jnp.where(allowed_pairs(lengths, query_rows.shape[0])[None], raw_scores, -1000000000.0)


def attend_row(scan_item):
    query_rows, key_rows, value_rows, lengths = scan_item
    scores = row_scores(query_rows, key_rows, lengths)
    row_max = jnp.max(scores, axis=-1, keepdims=True)
    exp_scores = jnp.exp(scores - row_max)
    row_total = jnp.sum(exp_scores, axis=-1, keepdims=True)
    softmax_low = (exp_scores / row_total).astype(jnp.bfloat16)
    mixed_rows = jnp.einsum(
        "hqk,khd->qhd", softmax_low, value_rows, preferred_element_type=jnp.float32
    )
    return (mixed_rows.astype(jnp.bfloat16), (row_max + jnp.log(row_total))[..., 0])


def attend_back(scan_item):
    query_rows, key_rows, value_rows, lengths, log_total, mixed_grad = scan_item
    scale = query_rows.shape[2] ** (-0.5)
    scores = row_scores(query_rows, key_rows, lengths)
    softmax_out = jnp.exp(scores - log_total[..., None])
    prob_grad = jnp.einsum(
        "qhd,khd->hqk", mixed_grad, value_rows, preferred_element_type=jnp.float32
    )
    inner_sum = jnp.sum(softmax_out * prob_grad, axis=-1, keepdims=True)
    score_grad = (softmax_out * (prob_grad - inner_sum)).astype(jnp.bfloat16)
    query_grad = (
        jnp.einsum("hqk,khd->qhd", score_grad, key_rows, preferred_element_type=jnp.float32) * scale
    )
    key_grad = (
        jnp.einsum("hqk,qhd->khd", score_grad, query_rows, preferred_element_type=jnp.float32)
        * scale
    )
    value_grad = jnp.einsum(
        "hqk,qhd->khd",
        softmax_out.astype(jnp.bfloat16),
        mixed_grad,
        preferred_element_type=jnp.float32,
    )
    return (
        query_grad.astype(jnp.bfloat16),
        key_grad.astype(jnp.bfloat16),
        value_grad.astype(jnp.bfloat16),
    )


def contract_first(left_arr, right_arr):
    return lax.dot_general(
        left_arr, right_arr, (((0,), (0,)), ((), ())), preferred_element_type=jnp.float32
    )


def contract_last(left_arr, right_arr):
    return lax.dot_general(
        left_arr, right_arr, (((1,), (1,)), ((), ())), preferred_element_type=jnp.float32
    )


def shards(
    inputs,
    doc_lengths,
    attn_gain,
    attn_shift,
    qkv_weight,
    qv_bias,
    out_weight,
    out_bias,
    mlp_gain,
    mlp_shift,
    up_weight,
    up_bias,
    down_weight,
    down_bias,
    out_grad,
):
    local_rows = inputs.shape[0]
    row_count = doc_lengths.shape[0]
    tokens = local_rows * lax.axis_size("tensor")
    length = tokens // row_count
    head_width = out_weight.shape[0]
    head_count = head_width // HD
    row_shape = (row_count, length, head_count, HD)
    attn_gain32 = attn_gain.astype(jnp.float32)
    attn_shift32 = attn_shift.astype(jnp.float32)
    mlp_gain32 = mlp_gain.astype(jnp.float32)
    mlp_shift32 = mlp_shift.astype(jnp.float32)

    def project(gathered):
        joined = jnp.einsum("td,dch->tch", gathered, qkv_weight, preferred_element_type=jnp.float32)
        query_rows = (joined[:, 0] + qv_bias[0]).astype(jnp.bfloat16)
        key_rows = joined[:, 1].astype(jnp.bfloat16)
        value_rows = (joined[:, 2] + qv_bias[1]).astype(jnp.bfloat16)
        return (query_rows, key_rows, value_rows)

    def attention(query_rows, key_rows, value_rows):
        mixed_rows, log_total = lax.map(
            attend_row,
            (
                query_rows.reshape(row_shape),
                key_rows.reshape(row_shape),
                value_rows.reshape(row_shape),
                doc_lengths,
            ),
        )
        return (mixed_rows.reshape(tokens, head_width), log_total)

    def hidden_layer(gathered):
        pre_act = jnp.dot(gathered, up_weight, preferred_element_type=jnp.float32) + up_bias
        return (pre_act, jax.nn.gelu(pre_act, approximate=True).astype(jnp.bfloat16))

    inputs32 = inputs.astype(jnp.float32)
    attn_rows = lax.all_gather(
        layer_norm(inputs32, attn_gain32, attn_shift32).astype(jnp.bfloat16),
        "tensor",
        axis=0,
        tiled=True,
    )
    query_rows, key_rows, value_rows = project(attn_rows)
    heads_out, log_total = attention(query_rows, key_rows, value_rows)
    attn_sum = lax.psum_scatter(
        jnp.dot(heads_out, out_weight, preferred_element_type=jnp.float32),
        "tensor",
        scatter_dimension=0,
        tiled=True,
    )
    middle = inputs32 + attn_sum + out_bias
    mlp_rows = lax.all_gather(
        layer_norm(middle, mlp_gain32, mlp_shift32).astype(jnp.bfloat16),
        "tensor",
        axis=0,
        tiled=True,
    )
    pre_act, hidden = hidden_layer(mlp_rows)
    mlp_sum = lax.psum_scatter(
        jnp.dot(hidden, down_weight, preferred_element_type=jnp.float32).astype(jnp.bfloat16),
        "tensor",
        scatter_dimension=0,
        tiled=True,
    ).astype(jnp.float32)
    outputs = middle + mlp_sum + down_bias
    grad32 = out_grad.astype(jnp.float32)
    down_bias_grad = jnp.sum(grad32, axis=0)
    grad_rows = lax.all_gather(out_grad, "tensor", axis=0, tiled=True)
    mlp_rows = lax.all_gather(
        layer_norm(middle, mlp_gain32, mlp_shift32).astype(jnp.bfloat16),
        "tensor",
        axis=0,
        tiled=True,
    )
    pre_act, hidden = hidden_layer(mlp_rows)
    down_weight_grad = contract_first(hidden, grad_rows)
    hidden_grad = contract_last(grad_rows, down_weight)
    gelu_value, gelu_pull = jax.vjp(
        lambda value_in: jax.nn.gelu(value_in, approximate=True), pre_act
    )
    pre_grad = gelu_pull(hidden_grad)[0].astype(jnp.bfloat16)
    up_bias_grad = jnp.sum(pre_grad, axis=0, dtype=jnp.float32)
    up_weight_grad = contract_first(mlp_rows, pre_grad)
    mlp_norm_grad = lax.psum_scatter(
        contract_last(pre_grad, up_weight), "tensor", scatter_dimension=0, tiled=True
    )
    norm_value, second_pull = jax.vjp(layer_norm, middle, mlp_gain32, mlp_shift32)
    middle_part, mlp_gain_grad, mlp_shift_grad = second_pull(mlp_norm_grad)
    middle_grad = grad32 + middle_part
    out_bias_grad = jnp.sum(middle_grad, axis=0)
    middle_rows = lax.all_gather(middle_grad.astype(jnp.bfloat16), "tensor", axis=0, tiled=True)
    attn_rows = lax.all_gather(
        layer_norm(inputs32, attn_gain32, attn_shift32).astype(jnp.bfloat16),
        "tensor",
        axis=0,
        tiled=True,
    )
    query_rows, key_rows, value_rows = project(attn_rows)
    heads_out, log_total = attention(query_rows, key_rows, value_rows)
    out_weight_grad = contract_first(heads_out, middle_rows)
    mixed_grad = contract_last(middle_rows, out_weight).astype(jnp.bfloat16)
    query_grad, key_grad, value_grad = lax.map(
        attend_back,
        (
            query_rows.reshape(row_shape),
            key_rows.reshape(row_shape),
            value_rows.reshape(row_shape),
            doc_lengths,
            log_total,
            mixed_grad.reshape(row_shape),
        ),
    )
    query_grad = query_grad.reshape(tokens, head_width)
    value_grad = value_grad.reshape(tokens, head_width)
    joined_grad = jnp.stack([query_grad, key_grad.reshape(tokens, head_width), value_grad], axis=1)
    qv_bias_grad = jnp.stack(
        [
            jnp.sum(query_grad, axis=0, dtype=jnp.float32),
            jnp.sum(value_grad, axis=0, dtype=jnp.float32),
        ]
    )
    qkv_weight_grad = jnp.einsum(
        "td,tch->dch", attn_rows, joined_grad, preferred_element_type=jnp.float32
    )
    attn_norm_grad = lax.psum_scatter(
        jnp.einsum("tch,dch->td", joined_grad, qkv_weight, preferred_element_type=jnp.float32),
        "tensor",
        scatter_dimension=0,
        tiled=True,
    )
    first_value, first_pull = jax.vjp(layer_norm, inputs32, attn_gain32, attn_shift32)
    input_part, attn_gain_grad, attn_shift_grad = first_pull(attn_norm_grad)
    input_grad = middle_grad + input_part
    shared = lax.psum(
        (
            attn_gain_grad,
            attn_shift_grad,
            out_bias_grad,
            mlp_gain_grad,
            mlp_shift_grad,
            down_bias_grad,
        ),
        ("dp", "tensor"),
    )
    (
        qkv_weight_grad,
        qv_bias_grad,
        out_weight_grad,
        up_weight_grad,
        up_bias_grad,
        down_weight_grad,
    ) = lax.psum(
        (
            qkv_weight_grad,
            qv_bias_grad,
            out_weight_grad,
            up_weight_grad,
            up_bias_grad,
            down_weight_grad,
        ),
        "dp",
    )
    return (
        outputs.astype(jnp.bfloat16),
        input_grad,
        shared[0],
        shared[1],
        qkv_weight_grad,
        qv_bias_grad,
        out_weight_grad,
        shared[2],
        shared[3],
        shared[4],
        up_weight_grad,
        up_bias_grad,
        down_weight_grad,
        shared[5],
    )


def solution(mesh):
    return jax.shard_map(
        shards,
        mesh=mesh,
        in_specs=(
            P(("dp", "tensor"), None),
            P("dp", None),
            P(),
            P(),
            P(None, None, "tensor"),
            P(None, "tensor"),
            P("tensor", None),
            P(),
            P(),
            P(),
            P(None, "tensor"),
            P("tensor"),
            P("tensor", None),
            P(),
            P(("dp", "tensor"), None),
        ),
        out_specs=(
            P(("dp", "tensor"), None),
            P(("dp", "tensor"), None),
            P(),
            P(),
            P(None, None, "tensor"),
            P(None, "tensor"),
            P("tensor", None),
            P(),
            P(),
            P(),
            P(None, "tensor"),
            P("tensor"),
            P("tensor", None),
            P(),
        ),
        check_vma=False,
    )
```

profile of v0, /device:TPU:0, one launch (start us, length us, event | category | flops | bytes accessed | tf_op | source)
XLA Modules:
  0.0 1738.7 jit_solution(4938154079184921427)
XLA Ops:
  15.3 57.2 %all-gather.5.cloned.1.call-done = bf16[2048,2048]{1,0:T(8,128)(2,1)} async-done(((bf16[256,2048]{1,0:T(8,128)(2,1)}), bf16[2048,2048]{1,0:T(8,128)(2,1)}) %all-gather.5.cloned.1.call-update) | async-done | bytes 8388624 | tf_op jit(solution)/shard_map/all_gather | solution.py:140
  72.4 9.0 fusion.105
  103.5 39.0 %while.36 = (s32[]{:T(128)}, bf16[2,1024,2,128]{3,2,1,0:T(2,128)(2,1)}, bf16[2,1024,2,128]{1,3,2,0:T(8,128)(2,1)}, s32[2,8]{1,0:T(2,128)S(1)}, bf16[2,1024,2,128...) while((s32[]{:T(128)}, bf16[2,1024,2,128]{3,2,1,0:T(2,128)(2,1)}, ...), condition=%wide.region_7.8_spmd, body=%wide.region_2.7_spmd.sunk | while | flops 1089757184 | bytes 23094540 | solution.py:124
  142.5 9.6 fusion.124
  152.8 115.4 %reduce-scatter.5.cloned.1.call-done = f32[256,2048]{1,0:T(8,128)} async-done(((f32[2048,2048]{1,0:T(8,128)}), f32[256,2048]{1,0:T(8,128)}) %reduce-scatter.5.cloned.1.call-update) | async-done | bytes 2097168 | tf_op jit(solution)/shard_map/reduce_scatter | solution.py:148
  273.9 53.9 %all-gather.7.cloned.1.call-done = bf16[2048,2048]{1,0:T(8,128)(2,1)} async-done(((bf16[256,2048]{1,0:T(8,128)(2,1)}), bf16[2048,2048]{1,0:T(8,128)(2,1)}) %all-gather.7.cloned.1.call-update) | async-done | bytes 8388624 | tf_op jit(solution)/shard_map/all_gather | solution.py:155
  327.8 14.5 fusion.148
  342.3 41.7 %all-gather.9.cloned.1.call-done = bf16[2048,2048]{1,0:T(8,128)(2,1)} async-done(((bf16[256,2048]{1,0:T(8,128)(2,1)}), bf16[2048,2048]{1,0:T(8,128)(2,1)}) %all-gather.9.cloned.1.call-update) | async-done | bytes 8388624 | tf_op jit(solution)/shard_map/all_gather | solution.py:171
  384.0 20.8 %convert_reduce_fusion.3 = (f32[1024]{0:T(1024)}, bf16[2048,1024]{1,0:T(8,128)(2,1)S(1)}) fusion(f32[2048,1024]{1,0:T(8,128)} %fusion.148, f32[1024]{0:T(1024)S(1)} %convert_element_type.153, bf16[2048,2048]{1,0:T(8,128)(2,1)} %all-gather.9.cloned.1.call-done, bf16[1024,2048]{1,0:T(8,128)(2,1)} %param.33), kind=kOutput, calls=%fused_computation.120 | convolution fusion | flops 8638168064 | bytes 25174016 | tf_op jit(solution)/shard_map/dot_general | solution.py:82
  406.8 11.9 fusion.149
  418.8 15.7 convolution_convert_fusion
  435.2 99.6 %reduce-scatter.9.cloned.1.call-done = f32[256,2048]{1,0:T(8,128)} async-done(((f32[2048,2048]{1,0:T(8,128)}), f32[256,2048]{1,0:T(8,128)}) %reduce-scatter.9.cloned.1.call-update) | async-done | bytes 2097168 | tf_op jit(solution)/shard_map/reduce_scatter | solution.py:187
  538.3 71.7 %reduce-scatter.7.cloned.1.call-done = bf16[256,2048]{1,0:T(8,128)(2,1)} async-done(((bf16[2048,2048]{1,0:T(8,128)(2,1)}), bf16[256,2048]{1,0:T(8,128)(2,1)}) %reduce-scatter.7.cloned.1.call-update) | async-done | bytes 1048592 | tf_op jit(solution)/shard_map/reduce_scatter | solution.py:162
  618.6 28.1 %while.37 = (s32[]{:T(128)}, bf16[2,1024,2,128]{3,2,1,0:T(2,128)(2,1)}, f32[2,2,1024]{2,1,0:T(2,128)S(1)}, bf16[2,1024,2,128]{1,3,2,0:T(8,128)(2,1)}, s32[2,8]{1...) while((s32[]{:T(128)}, ...), condition=%wide.region_20.21_spmd, body=%wide.region_15.20_spmd.sunk | while | flops 1102337024 | bytes 37823796 | solution.py:124
  646.7 24.8 %all-gather.11.cloned.1.call-done = bf16[2048,2048]{1,0:T(8,128)(2,1)} async-done(((bf16[256,2048]{1,0:T(8,128)(2,1)}), bf16[2048,2048]{1,0:T(8,128)(2,1)}) %all-gather.11.cloned.1.call-update) | async-done | bytes 8388624 | tf_op jit(solution)/shard_map/all_gather | solution.py:194
  682.1 44.8 %while.38 = (s32[]{:T(128)}, bf16[2,1024,2,128]{1,3,2,0:T(8,128)(2,1)}, bf16[2,1024,2,128]{3,2,1,0:T(2,128)(2,1)}, bf16[2,1024,2,128]{1,3,2,0:T(8,128)(2,1)}, bf...) while((s32[]{:T(128)}, ...), condition=%wide.region_25.26_spmd, body=%wide.region_21.25_spmd.sunk | while | flops 2720289792 | bytes 88148360 | solution.py:205
  746.1 9.7 convolution_bitcast_fusion
  756.0 15.0 fusion.150
  771.0 21.1 %fusion.132 = f32[1024,2048]{1,0:T(8,128)} fusion(bf16[2048,2048]{1,0:T(8,128)(2,1)} %all-gather.9.cloned.1.call-done, f32[2048,1024]{1,0:T(8,128)} %fusion.148, f32[1024]{0:T(1024)S(1)} %copy-done.36), kind=kOutput, calls=%fused_computation.181 | convolution fusion | flops 8610906112 | bytes 25169920 | tf_op jit(solution)/shard_map/dot_general | solution.py:76
  799.4 9.0 fusion.103
  811.3 12.7 all-reduce.1
  824.0 48.0 %reduce-scatter.11.cloned.1.call-done = f32[256,2048]{1,0:T(8,128)} async-done(((f32[2048,2048]{1,0:T(8,128)}), f32[256,2048]{1,0:T(8,128)}) %reduce-scatter.11.cloned.1.call-update) | async-done | bytes 2097168 | tf_op jit(solution)/shard_map/reduce_scatter | solution.py:228
  880.3 44.2 %all-reduce = (f32[2048]{0:T(1024)}, f32[2048]{0:T(1024)}, f32[2048]{0:T(1024)}, f32[2048]{0:T(1024)}, f32[2048]{0:T(1024)}, /*index=5*/f32[2048]{0:T(1024)}) all-reduce(f32[2048]{0:T(1024)S(1)} %get-tuple-element.215, f32[2048]{0:T(1024)S(1)} %get-tuple-element.218, ...), channel_id=1, replica_groups=mesh['dp'=4,'tensor'=8] {'dp','tensor'}, use_global_device_ids=true, to_apply=%region_30.31 | all-reduce | flops 12288 | bytes 98304 | tf_op jit(solution)/shard_map/psum | solution.py:237
  924.5 789.6 %all-reduce.5.cloned.1.call-done = (f32[2048,3,256]{2,0,1:T(8,128)}, f32[256,2048]{1,0:T(8,128)}, f32[2048,1024]{1,0:T(8,128)}, f32[1024,2048]{1,0:T(8,128)}) async-done(((f32[2048,3,256]{2,0,1:T(8,128)}, f32[256,2048]{1,0:T(8,128)}, f32[2048,1024]{1,0:T(8,128)}, f32[1024,2048]{1,0:T(8,128)}), (f32[2048,3,256]{2,0,1:T(8,128)}, f32[256,2048]{1,0:T(8,128)}, f32[2048,1024]{1,0:T(8,128)}, ...) | async-done | bytes 25165840 | tf_op jit(solution)/shard_map/psum | solution.py:255
  (244 shorter events, 227.8 us)
Async XLA Ops:
  7.2 65.3 %copy-start = (bf16[2048,3,256]{2,0,1:T(8,128)(2,1)S(1)}, bf16[2048,3,256]{2,0,1:T(8,128)(2,1)}, u32[]{:S(2)}) copy-start(bf16[2048,3,256]{2,0,1:T(8,128)(2,1)} %param.25) | copy-start | bytes 9437188
  7.2 8.0 copy-start.37
  7.2 65.2 %all-gather.5.cloned.1.call-start = ((), (), s32[]{:S(2)}) async-start(), calls=%async_computation.4 | async-start | bytes 9437184 | tf_op jit(solution)/shard_map/all_gather | solution.py:140
  15.2 253.1 %reduce-scatter.5.cloned.1.call-start = ((), (), s32[]{:S(2)}) async-start(), calls=%async_computation.5 | async-start | bytes 18874368 | tf_op jit(solution)/shard_map/reduce_scatter | solution.py:148
  95.8 7.7 copy-start.40
  152.1 175.7 %all-gather.7.cloned.1.call-start = ((), (), s32[]{:S(2)}) async-start(), calls=%async_computation.6 | async-start | bytes 9437184 | tf_op jit(solution)/shard_map/all_gather | solution.py:155
  273.2 110.7 %all-gather.9.cloned.1.call-start = ((), (), s32[]{:S(2)}) async-start(), calls=%async_computation.8 | async-start | bytes 9437184 | tf_op jit(solution)/shard_map/all_gather | solution.py:171
  273.8 261.0 %reduce-scatter.9.cloned.1.call-start = ((), (), s32[]{:S(2)}) async-start(), calls=%async_computation.9 | async-start | bytes 18874368 | tf_op jit(solution)/shard_map/reduce_scatter | solution.py:187
  273.9 144.9 %copy-start.35 = (f32[1024]{0:T(1024)}, f32[1024]{0:T(1024)S(1)}, u32[]{:S(2)}) copy-start(f32[1024]{0:T(1024)S(1)} %convert_element_type.153) | copy-start | bytes 12292
  384.0 22.8 %copy-start.39 = (bf16[2048,1024]{1,0:T(8,128)(2,1)S(1)}, bf16[2048,1024]{1,0:T(8,128)(2,1)}, u32[]{:S(2)}) copy-start(bf16[2048,1024]{1,0:T(8,128)(2,1)} %param.31) | copy-start | bytes 12582916
  418.7 191.3 %reduce-scatter.7.cloned.1.call-start = ((), (), s32[]{:S(2)}) async-start(), calls=%async_computation.7 | async-start | bytes 9437184 | tf_op jit(solution)/shard_map/reduce_scatter | solution.py:162
  434.5 237.0 %all-gather.11.cloned.1.call-start = ((), (), s32[]{:S(2)}) async-start(), calls=%async_computation.10 | async-start | bytes 9437184 | tf_op jit(solution)/shard_map/all_gather | solution.py:194
  617.0 255.1 %reduce-scatter.11.cloned.1.call-start = ((), (), s32[]{:S(2)}) async-start(), calls=%async_computation.11 | async-start | bytes 18874368 | tf_op jit(solution)/shard_map/reduce_scatter | solution.py:228
  755.9 15.1 copy-start.36
  755.9 958.2 %all-reduce.5.cloned.1.call-start = ((), (), s32[]{:S(2)}) async-start(), calls=%async_computation.12 | async-start | bytes 50331648 | tf_op jit(solution)/shard_map/psum | solution.py:255
  756.0 43.4 %slice-start.2 = ((s8[8388608]{0:T(1024)(128)(4,1)}), s8[4194304]{0:T(1024)(128)(4,1)S(1)}, s32[]{:S(2)}) async-start(s8[8388608]{0:T(1024)(128)(4,1)} %bitcast.213), calls=%async_computation.15 | async-start | bytes 8388608
  771.0 21.1 %copy-start.12 = (bf16[2,1024,2,128]{3,2,1,0:T(2,128)(2,1)S(1)}, bf16[2,1024,2,128]{3,2,1,0:T(2,128)(2,1)}, u32[]{:S(2)}) copy-start(bf16[2,1024,2,128]{3,2,1,0:T(2,128)(2,1)} %get-tuple-element.143) | copy-start | bytes 3145732
  771.0 28.4 %slice-start.3 = ((s8[8388608]{0:T(1024)(128)(4,1)}), s8[4194304]{0:T(1024)(128)(4,1)S(1)}, s32[]{:S(2)}) async-start(s8[8388608]{0:T(1024)(128)(4,1)} %bitcast.213), calls=%async_computation.16 | async-start | bytes 8388608
  808.3 63.7 %copy-start.19 = (f32[2048]{0:T(1024)S(1)}, f32[2048]{0:T(1024)}, u32[]{:S(2)}) copy-start(f32[2048]{0:T(1024)} %copy-done.18) | copy-start | bytes 24580
  808.3 63.7 %copy-start.21 = (f32[256]{0:T(256)S(1)}, f32[256]{0:T(256)}, u32[]{:S(2)}) copy-start(f32[256]{0:T(256)} %copy-done.20) | copy-start | bytes 3076
  808.4 66.2 %copy-start.29 = (f32[256]{0:T(256)S(1)}, f32[256]{0:T(256)}, u32[]{:S(2)}) copy-start(f32[256]{0:T(256)} %copy-done.28) | copy-start | bytes 3076
  808.4 66.2 %copy-start.25 = (f32[256]{0:T(256)S(1)}, f32[256]{0:T(256)}, u32[]{:S(2)}) copy-start(f32[256]{0:T(256)} %copy-done.24) | copy-start | bytes 3076
  808.4 69.3 %copy-start.27 = (f32[256]{0:T(256)S(1)}, f32[256]{0:T(256)}, u32[]{:S(2)}) copy-start(f32[256]{0:T(256)} %copy-done.26) | copy-start | bytes 3076
  1714.1 8.9 copy-start.11
  (35 other events, 106.5 us)
Sparse Core Ops, SparseCore 0:
  15.3 57.0 all-gather.4
  152.3 115.9 reduce-scatter.4
  273.4 54.3 all-gather.6
  329.5 54.3 all-gather.8
  418.8 115.9 reduce-scatter.8
  538.7 71.2 reduce-scatter.6
  617.1 54.3 all-gather.10
  756.0 115.9 reduce-scatter.10
  876.3 837.7 all-reduce.4
where the time goes:
time: 1750 us; the launch traced here: 1740 us
  waiting for transfers between devices  1300 us (74%)
  matrix products  216 us (12%)
  local copies, waits for them, and re-layouts  94.8 us (5%)
  blocking collectives  56.8 us (3%)
  other arithmetic  52 us (3%)
    psum x1, waiting for transfers between devices, shards(): lax.psum((qkv_weight_grad, qv_bias_grad, out_weight_grad, up_weight_grad,...  790 us
    reduce_scatter x1, waiting for transfers between devices, shards(): lax.psum_scatter(jnp.dot(heads_out, out_weight, preferred_element_type=jn...  115 us
    reduce_scatter x1, waiting for transfers between devices, shards(): lax.psum_scatter(contract_last(pre_grad, up_weight), 'tensor', scatter_di...  99.6 us
    reduce_scatter x1, waiting for transfers between devices, shards(): lax.psum_scatter(jnp.dot(hidden, down_weight, preferred_element_type=jnp....  71.7 us
    all_gather x1, waiting for transfers between devices, shards(): lax.all_gather(layer_norm(inputs32, attn_gain32, attn_shift32).astype(jnp...  57.2 us
    all_gather x1, waiting for transfers between devices, shards(): lax.all_gather(layer_norm(middle, mlp_gain32, mlp_shift32).astype(jnp.bfl...  53.9 us
    reduce_scatter x1, waiting for transfers between devices, shards(): lax.psum_scatter(jnp.einsum('tch,dch->td', joined_grad, qkv_weight, prefe...  48 us
    psum x1, blocking collectives, shards(): lax.psum((attn_gain_grad, attn_shift_grad, out_bias_grad, mlp_gain_grad,...  44.2 us
  transfers between devices with their start and end apart: 9, of which 9 were waited for; matrix products, arithmetic and copies ran while one was open for 7% of the time, Pallas kernels for 0%

commit v1 on v0

--- a/solution.py
+++ b/solution.py
@@ -5,6 +5,19 @@
 
 HD = 128
 NORM_EPS = 1e-05
+
+
+def collect(x, axis, dim):
+    ways = lax.axis_size(axis)
+    up = [(d, (d + 1) % ways) for d in range(ways)]
+    down = [(d, (d - 1) % ways) for d in range(ways)]
+    earlier, later = ([x], [x])
+    for _ in range(ways // 2):
+        earlier.append(lax.ppermute(earlier[-1], axis, up))
+    for _ in range((ways - 1) // 2):
+        later.append(lax.ppermute(later[-1], axis, down))
+    line = jnp.concatenate([*earlier[::-1], *later[1:]], axis=dim)
+    return jnp.roll(line, (lax.axis_index(axis) - ways // 2) * x.shape[dim], axis=dim)
 
 
 def layer_norm(values, gain_vec, shift_vec):
@@ -137,11 +150,8 @@
         return (pre_act, jax.nn.gelu(pre_act, approximate=True).astype(jnp.bfloat16))
 
     inputs32 = inputs.astype(jnp.float32)
-    attn_rows = lax.all_gather(
-        layer_norm(inputs32, attn_gain32, attn_shift32).astype(jnp.bfloat16),
-        "tensor",
-        axis=0,
-        tiled=True,
+    attn_rows = collect(
+        layer_norm(inputs32, attn_gain32, attn_shift32).astype(jnp.bfloat16), "tensor", 0
     )
     query_rows, key_rows, value_rows = project(attn_rows)
     heads_out, log_total = attention(query_rows, key_rows, value_rows)

time: 1750 us -> 1850 us (1.057)
  waiting for transfers between devices: 1300 us -> 1340 us
  local copies, waits for them, and re-layouts: 94.8 us -> 129 us
    ppermute x0 -> x7, waiting for transfers between devices: none -> 101 us  [the longest x4 101 us: collect(): earlier.append(lax.ppermute(earlier[-1], axis, up))]
    all_gather x1, waiting for transfers between devices: 57.2 us -> 0.01 us  [shards(): lax.all_gather(layer_norm(inputs32, attn_gain32, attn_shift32).astype(jnp...]
    unnamed x90 -> x113, local copies, waits for them, and re-layouts: 28.3 us -> 45 us
  transfers between devices with their start and end apart: 9 -> 16, of which waited for: 9 -> 12; matrix products, arithmetic and copies ran while one was open for 7% -> 9% of each run, Pallas kernels for 0% -> 0%
where the time goes in v1:
time: 1850 us; the launch traced here: 1840 us
  waiting for transfers between devices  1340 us (72%)
  matrix products  224 us (12%)
  local copies, waits for them, and re-layouts  129 us (7%)
  blocking collectives  56.8 us (3%)
  other arithmetic  55.9 us (3%)
    psum x1, waiting for transfers between devices, shards(): lax.psum((qkv_weight_grad, qv_bias_grad, out_weight_grad, up_weight_grad,...  790 us
    reduce_scatter x1, waiting for transfers between devices, shards(): lax.psum_scatter(jnp.dot(heads_out, out_weight, preferred_element_type=jn...  121 us
    ppermute x4, waiting for transfers between devices, collect(): earlier.append(lax.ppermute(earlier[-1], axis, up))  101 us
    reduce_scatter x1, waiting for transfers between devices, shards(): lax.psum_scatter(contract_last(pre_grad, up_weight), 'tensor', scatter_di...  99.7 us
    reduce_scatter x1, waiting for transfers between devices, shards(): lax.psum_scatter(jnp.dot(hidden, down_weight, preferred_element_type=jnp....  71.7 us
    all_gather x1, waiting for transfers between devices, shards(): lax.all_gather(layer_norm(middle, mlp_gain32, mlp_shift32).astype(jnp.bfl...  53.9 us
    reduce_scatter x1, waiting for transfers between devices, shards(): lax.psum_scatter(jnp.einsum('tch,dch->td', joined_grad, qkv_weight, prefe...  48 us
    unnamed x113, local copies, waits for them, and re-layouts  45 us
  transfers between devices with their start and end apart: 16, of which 12 were waited for; matrix products, arithmetic and copies ran while one was open for 9% of the time, Pallas kernels for 0%

profile of v1, /device:TPU:0, one launch (start us, length us, event | category | flops | bytes accessed | tf_op | source)
XLA Modules:
  0.0 1839.5 jit_solution(4828554339124537554)
XLA Ops:
  15.7 19.2 %collective-permute-done = bf16[256,2048]{1,0:T(8,128)(2,1)S(1)} collective-permute-done((bf16[256,2048]{1,0:T(8,128)(2,1)}, bf16[256,2048]{1,0:T(8,128)(2,1)S(1)}, u32[]{:S(2)}, u32[]{:S(2)}) %collective-permute-start) | collective-permute-done | bytes 1048608 | tf_op jit(solution)/shard_map/ppermute | solution.py:16
  38.8 33.3 %collective-permute-done.1 = bf16[256,2048]{1,0:T(8,128)(2,1)S(1)} collective-permute-done((bf16[256,2048]{1,0:T(8,128)(2,1)S(1)}, bf16[256,2048]{1,0:T(8,128)(2,1)S(1)}, u32[]{:S(2)}, u32[]{:S(2)}) %collective-permute-start.1) | collective-permute-done | bytes 1048608 | tf_op jit(solution)/shard_map/ppermute | solution.py:16
  80.3 27.4 %collective-permute-done.2 = bf16[256,2048]{1,0:T(8,128)(2,1)} collective-permute-done((bf16[256,2048]{1,0:T(8,128)(2,1)S(1)}, bf16[256,2048]{1,0:T(8,128)(2,1)}, u32[]{:S(2)}, u32[]{:S(2)}) %collective-permute-start.2) | collective-permute-done | bytes 1048608 | tf_op jit(solution)/shard_map/ppermute | solution.py:16
  111.3 20.9 %collective-permute-done.3 = bf16[256,2048]{1,0:T(8,128)(2,1)} collective-permute-done((bf16[256,2048]{1,0:T(8,128)(2,1)}, bf16[256,2048]{1,0:T(8,128)(2,1)}, u32[]{:S(2)}, u32[]{:S(2)}) %collective-permute-start.3) | collective-permute-done | bytes 1048608 | tf_op jit(solution)/shard_map/ppermute | solution.py:16
  192.7 43.6 %while.36 = (s32[]{:T(128)}, bf16[2,1024,2,128]{3,2,1,0:T(2,128)(2,1)}, bf16[2,1024,2,128]{3,1,2,0:T(8,128)(2,1)}, s32[2,8]{1,0:T(2,128)S(1)}, bf16[2,1024,2,128...) while((s32[]{:T(128)}, bf16[2,1024,2,128]{3,2,1,0:T(2,128)(2,1)}, ...), condition=%wide.region_7.8_spmd, body=%wide.region_2.7_spmd.sunk | while | flops 1089757184 | bytes 24142100 | solution.py:137
  246.6 121.1 %reduce-scatter.5.cloned.1.call-done = f32[256,2048]{1,0:T(8,128)} async-done(((f32[2048,2048]{1,0:T(8,128)}), f32[256,2048]{1,0:T(8,128)}) %reduce-scatter.5.cloned.1.call-update) | async-done | bytes 2097168 | tf_op jit(solution)/shard_map/reduce_scatter | solution.py:158
  373.4 53.9 %all-gather.5.cloned.1.call-done = bf16[2048,2048]{1,0:T(8,128)(2,1)} async-done(((bf16[256,2048]{1,0:T(8,128)(2,1)}), bf16[2048,2048]{1,0:T(8,128)(2,1)}) %all-gather.5.cloned.1.call-update) | async-done | bytes 8388624 | tf_op jit(solution)/shard_map/all_gather | solution.py:165
  427.2 14.6 fusion.143
  441.8 41.5 %all-gather.7.cloned.1.call-done = bf16[2048,2048]{1,0:T(8,128)(2,1)} async-done(((bf16[256,2048]{1,0:T(8,128)(2,1)}), bf16[2048,2048]{1,0:T(8,128)(2,1)}) %all-gather.7.cloned.1.call-update) | async-done | bytes 8388624 | tf_op jit(solution)/shard_map/all_gather | solution.py:181
  483.4 20.8 %convert_reduce_fusion.3 = (f32[1024]{0:T(1024)}, bf16[2048,1024]{1,0:T(8,128)(2,1)S(1)}) fusion(f32[2048,1024]{1,0:T(8,128)} %fusion.143, f32[1024]{0:T(1024)S(1)} %convert_element_type.163, bf16[2048,2048]{1,0:T(8,128)(2,1)} %all-gather.7.cloned.1.call-done, bf16[1024,2048]{1,0:T(8,128)(2,1)} %param.33), kind=kOutput, calls=%fused_computation.120 | convolution fusion | flops 8638168064 | bytes 25174016 | tf_op jit(solution)/shard_map/dot_general | solution.py:95
  506.2 12.0 fusion.144
  518.3 15.7 convolution_convert_fusion
  534.7 99.7 %reduce-scatter.9.cloned.1.call-done = f32[256,2048]{1,0:T(8,128)} async-done(((f32[2048,2048]{1,0:T(8,128)}), f32[256,2048]{1,0:T(8,128)}) %reduce-scatter.9.cloned.1.call-update) | async-done | bytes 2097168 | tf_op jit(solution)/shard_map/reduce_scatter | solution.py:197
  637.9 71.7 %reduce-scatter.7.cloned.1.call-done = bf16[256,2048]{1,0:T(8,128)(2,1)} async-done(((bf16[2048,2048]{1,0:T(8,128)(2,1)}), bf16[256,2048]{1,0:T(8,128)(2,1)}) %reduce-scatter.7.cloned.1.call-update) | async-done | bytes 1048592 | tf_op jit(solution)/shard_map/reduce_scatter | solution.py:172
  725.6 27.7 %while.37 = (s32[]{:T(128)}, bf16[2,1024,2,128]{3,2,1,0:T(2,128)(2,1)}, f32[2,2,1024]{2,1,0:T(2,128)S(1)}, bf16[2,1024,2,128]{3,1,2,0:T(8,128)(2,1)}, s32[2,8]{1...) while((s32[]{:T(128)}, ...), condition=%wide.region_20.21_spmd, body=%wide.region_15.20_spmd.sunk | while | flops 1102337024 | bytes 37823796 | solution.py:137
  753.3 17.7 all-gather.11.cloned.1.call-done
  781.6 44.5 %while.38 = (s32[]{:T(128)}, bf16[2,1024,2,128]{1,3,2,0:T(8,128)(2,1)}, bf16[2,1024,2,128]{3,2,1,0:T(2,128)(2,1)}, bf16[2,1024,2,128]{1,3,2,0:T(8,128)(2,1)}, bf...) while((s32[]{:T(128)}, ...), condition=%wide.region_25.26_spmd, body=%wide.region_21.25_spmd.sunk | while | flops 2720289792 | bytes 88148360 | solution.py:215
  846.5 9.8 convolution_bitcast_fusion
  856.4 15.0 fusion.145
  871.4 21.1 %fusion.130 = f32[1024,2048]{1,0:T(8,128)} fusion(bf16[2048,2048]{1,0:T(8,128)(2,1)} %all-gather.7.cloned.1.call-done, f32[2048,1024]{1,0:T(8,128)} %fusion.143, f32[1024]{0:T(1024)S(1)} %copy-done.40), kind=kOutput, calls=%fused_computation.204 | convolution fusion | flops 8610906112 | bytes 25169920 | tf_op jit(solution)/shard_map/dot_general | solution.py:89
  911.8 12.7 all-reduce.1
  924.5 48.0 %reduce-scatter.11.cloned.1.call-done = f32[256,2048]{1,0:T(8,128)} async-done(((f32[2048,2048]{1,0:T(8,128)}), f32[256,2048]{1,0:T(8,128)}) %reduce-scatter.11.cloned.1.call-update) | async-done | bytes 2097168 | tf_op jit(solution)/shard_map/reduce_scatter | solution.py:238
  980.7 44.2 %all-reduce = (f32[2048]{0:T(1024)}, f32[2048]{0:T(1024)}, f32[2048]{0:T(1024)}, f32[2048]{0:T(1024)}, f32[2048]{0:T(1024)}, /*index=5*/f32[2048]{0:T(1024)}) all-reduce(f32[2048]{0:T(1024)S(1)} %get-tuple-element.215, f32[2048]{0:T(1024)S(1)} %get-tuple-element.218, ...), channel_id=1, replica_groups=mesh['dp'=4,'tensor'=8] {'dp','tensor'}, use_global_device_ids=true, to_apply=%region_30.31 | all-reduce | flops 12288 | bytes 98304 | tf_op jit(solution)/shard_map/psum | solution.py:247
  1024.9 789.7 %all-reduce.5.cloned.1.call-done = (f32[2048,3,256]{2,0,1:T(8,128)}, f32[256,2048]{1,0:T(8,128)}, f32[2048,1024]{1,0:T(8,128)}, f32[1024,2048]{1,0:T(8,128)}) async-done(((f32[2048,3,256]{2,0,1:T(8,128)}, f32[256,2048]{1,0:T(8,128)}, f32[2048,1024]{1,0:T(8,128)}, f32[1024,2048]{1,0:T(8,128)}), (f32[2048,3,256]{2,0,1:T(8,128)}, f32[256,2048]{1,0:T(8,128)}, f32[2048,1024]{1,0:T(8,128)}, ...) | async-done | bytes 25165840 | tf_op jit(solution)/shard_map/psum | solution.py:265
  (292 shorter events, 314.0 us)
Async XLA Ops:
  7.2 138.1 %copy-start = (bf16[2048,3,256]{2,0,1:T(8,128)(2,1)S(1)}, bf16[2048,3,256]{2,0,1:T(8,128)(2,1)}, u32[]{:S(2)}) copy-start(bf16[2048,3,256]{2,0,1:T(8,128)(2,1)} %param.25) | copy-start | bytes 9437188
  7.2 157.4 %all-gather.9.cloned.1.call-start = ((), (), s32[]{:S(2)}) async-start(), calls=%async_computation.9 | async-start | bytes 9437184 | tf_op jit(solution)/shard_map/all_gather | solution.py:205
  8.8 133.3 %copy-start.24 = (f32[256]{0:T(256)}, f32[256]{0:T(256)S(1)}, u32[]{:S(2)}) copy-start(f32[256]{0:T(256)S(1)} %broadcast_multiply_fusion.1) | copy-start | bytes 3076
  11.1 131.1 %copy-start.26 = (f32[256]{0:T(256)}, f32[256]{0:T(256)S(1)}, u32[]{:S(2)}) copy-start(f32[256]{0:T(256)S(1)} %fusion.124) | copy-start | bytes 3076
  11.8 130.4 %copy-start.20 = (f32[2048]{0:T(1024)}, f32[2048]{0:T(1024)S(1)}, u32[]{:S(2)}) copy-start(f32[2048]{0:T(1024)S(1)} %convert_element_type.153) | copy-start | bytes 24580
  15.1 352.6 %reduce-scatter.5.cloned.1.call-start = ((), (), s32[]{:S(2)}) async-start(), calls=%async_computation.4 | async-start | bytes 18874368 | tf_op jit(solution)/shard_map/reduce_scatter | solution.py:158
  15.2 19.7 %collective-permute-start = (bf16[256,2048]{1,0:T(8,128)(2,1)}, bf16[256,2048]{1,0:T(8,128)(2,1)S(1)}, u32[]{:S(2)}, u32[]{:S(2)}) collective-permute-start(bf16[256,2048]{1,0:T(8,128)(2,1)} %fusion.109), channel_id=1, source_target_pairs={{0,1},{1,2},{2,3},{3,4},{4,5},{5,6},{6,7},{7,0},{8,9},{9,10},{10,1... | collective-permute-start | bytes 3145736 | tf_op jit(solution)/shard_map/ppermute | solution.py:16
  35.9 36.3 %collective-permute-start.1 = (bf16[256,2048]{1,0:T(8,128)(2,1)S(1)}, bf16[256,2048]{1,0:T(8,128)(2,1)S(1)}, u32[]{:S(2)}, u32[]{:S(2)}) collective-permute-start(bf16[256,2048]{1,0:T(8,128)(2,1)S(1)} %collective-permute-done), channel_id=1, source_target_pairs={{0,1},{1,2},{2,3},{3,4},{4,5},{5,6},{6,7},{7,0},{8,9},{9,10},{10,1... | collective-permute-start | bytes 3145736 | tf_op jit(solution)/shard_map/ppermute | solution.py:16
  38.8 41.1 %collective-permute-start.4 = (bf16[256,2048]{1,0:T(8,128)(2,1)}, bf16[256,2048]{1,0:T(8,128)(2,1)}, u32[]{:S(2)}, u32[]{:S(2)}) collective-permute-start(bf16[256,2048]{1,0:T(8,128)(2,1)} %fusion.109), channel_id=1, source_target_pairs={{0,7},{1,0},{2,1},{3,2},{4,3},{5,4},{6,5},{7,6},{8,15},{9,8},{10,9... | collective-permute-start | bytes 3145736 | tf_op jit(solution)/shard_map/ppermute | solution.py:18
  73.1 34.6 %collective-permute-start.2 = (bf16[256,2048]{1,0:T(8,128)(2,1)S(1)}, bf16[256,2048]{1,0:T(8,128)(2,1)}, u32[]{:S(2)}, u32[]{:S(2)}) collective-permute-start(bf16[256,2048]{1,0:T(8,128)(2,1)S(1)} %collective-permute-done.1), channel_id=1, source_target_pairs={{0,1},{1,2},{2,3},{3,4},{4,5},{5,6},{6,7},{7,0},{8,9},{9,10},{10,1... | collective-permute-start | bytes 3145736 | tf_op jit(solution)/shard_map/ppermute | solution.py:16
  80.0 29.8 %collective-permute-start.5 = (bf16[256,2048]{1,0:T(8,128)(2,1)}, bf16[256,2048]{1,0:T(8,128)(2,1)}, u32[]{:S(2)}, u32[]{:S(2)}) collective-permute-start(bf16[256,2048]{1,0:T(8,128)(2,1)} %collective-permute-done.4), channel_id=1, source_target_pairs={{0,7},{1,0},{2,1},{3,2},{4,3},{5,4},{6,5},{7,6},{8,15},{9,8},{10,9... | collective-permute-start | bytes 3145736 | tf_op jit(solution)/shard_map/ppermute | solution.py:18
  107.7 24.5 %collective-permute-start.3 = (bf16[256,2048]{1,0:T(8,128)(2,1)}, bf16[256,2048]{1,0:T(8,128)(2,1)}, u32[]{:S(2)}, u32[]{:S(2)}) collective-permute-start(bf16[256,2048]{1,0:T(8,128)(2,1)} %collective-permute-done.2), channel_id=1, source_target_pairs={{0,1},{1,2},{2,3},{3,4},{4,5},{5,6},{6,7},{7,0},{8,9},{9,10},{10,1... | collective-permute-start | bytes 3145736 | tf_op jit(solution)/shard_map/ppermute | solution.py:16
  109.7 29.5 %collective-permute-start.6 = (bf16[256,2048]{1,0:T(8,128)(2,1)}, bf16[256,2048]{1,0:T(8,128)(2,1)S(1)}, u32[]{:S(2)}, u32[]{:S(2)}) collective-permute-start(bf16[256,2048]{1,0:T(8,128)(2,1)} %collective-permute-done.5), channel_id=1, source_target_pairs={{0,7},{1,0},{2,1},{3,2},{4,3},{5,4},{6,5},{7,6},{8,15},{9,8},{10,9... | collective-permute-start | bytes 3145736 | tf_op jit(solution)/shard_map/ppermute | solution.py:18
  245.9 181.3 %all-gather.5.cloned.1.call-start = ((), (), s32[]{:S(2)}) async-start(), calls=%async_computation.5 | async-start | bytes 9437184 | tf_op jit(solution)/shard_map/all_gather | solution.py:165
  246.6 126.7 %copy-start.41 = (bf16[1024]{0:T(1024)(128)(2,1)S(1)}, bf16[1024]{0:T(1024)(128)(2,1)}, u32[]{:S(2)}) copy-start(bf16[1024]{0:T(1024)(128)(2,1)} %param.32) | copy-start | bytes 6148
  372.7 110.7 %all-gather.7.cloned.1.call-start = ((), (), s32[]{:S(2)}) async-start(), calls=%async_computation.7 | async-start | bytes 9437184 | tf_op jit(solution)/shard_map/all_gather | solution.py:181
  373.3 261.1 %reduce-scatter.9.cloned.1.call-start = ((), (), s32[]{:S(2)}) async-start(), calls=%async_computation.8 | async-start | bytes 18874368 | tf_op jit(solution)/shard_map/reduce_scatter | solution.py:197
  373.3 144.9 %copy-start.39 = (f32[1024]{0:T(1024)}, f32[1024]{0:T(1024)S(1)}, u32[]{:S(2)}) copy-start(f32[1024]{0:T(1024)S(1)} %convert_element_type.163) | copy-start | bytes 12292
  518.2 191.3 %reduce-scatter.7.cloned.1.call-start = ((), (), s32[]{:S(2)}) async-start(), calls=%async_computation.6 | async-start | bytes 9437184 | tf_op jit(solution)/shard_map/reduce_scatter | solution.py:172
  534.0 237.0 %all-gather.11.cloned.1.call-start = ((), (), s32[]{:S(2)}) async-start(), calls=%async_computation.10 | async-start | bytes 9437184 | tf_op jit(solution)/shard_map/all_gather | solution.py:204
  716.5 256.0 %reduce-scatter.11.cloned.1.call-start = ((), (), s32[]{:S(2)}) async-start(), calls=%async_computation.11 | async-start | bytes 18874368 | tf_op jit(solution)/shard_map/reduce_scatter | solution.py:238
  856.4 958.2 %all-reduce.5.cloned.1.call-start = ((), (), s32[]{:S(2)}) async-start(), calls=%async_computation.12 | async-start | bytes 50331648 | tf_op jit(solution)/shard_map/psum | solution.py:265
  908.9 66.2 %copy-start.27 = (f32[256]{0:T(256)S(1)}, f32[256]{0:T(256)}, u32[]{:S(2)}) copy-start(f32[256]{0:T(256)} %copy-done.26) | copy-start | bytes 3076
  908.9 69.2 %copy-start.31 = (f32[256]{0:T(256)S(1)}, f32[256]{0:T(256)}, u32[]{:S(2)}) copy-start(f32[256]{0:T(256)} %copy-done.30) | copy-start | bytes 3076
  (47 other events, 520.3 us)
Sparse Core Ops, SparseCore 0:
  15.3 78.7 all-gather.8
  246.1 121.6 reduce-scatter.4
  372.8 54.3 all-gather.4
  429.0 54.3 all-gather.6
  518.3 115.9 reduce-scatter.8
  638.2 71.2 reduce-scatter.6
  716.6 54.3 all-gather.10
  856.5 115.9 reduce-scatter.10
  976.8 837.7 all-reduce.4
